TPU v7x, 32 devices: a whole 2x2x4 slice. The times are simulated.
32 devices in a mesh: batch: 8 (over z, core), seq: 4 (over y, x).
Axes of the slice: x: 2, y: 2, z: 4, core: 2. Of those that a mesh axis runs over, the one named last changes fastest.
Arguments:
- token_cond: bfloat16 [16384, 768], P(('batch', 'seq')), parts along dimension 0, may hold values from -6 to 6
- atom_feat: bfloat16 [131072, 128], P(('batch', 'seq')), parts along dimension 0, may hold values from -16 to 16
- atom_counts: int32 [16384], P(('batch', 'seq')), parts along dimension 0, may hold values from 1 to 24, as said below
- w_token: bfloat16 [768, 128], replicated, may hold values from -0.21875 to 0.21875
- w_query: bfloat16 [128, 128], replicated, may hold values from -0.5 to 0.5
- w_key: bfloat16 [128, 128], replicated, may hold values from -0.5 to 0.5
- w_value: bfloat16 [128, 128], replicated, may hold values from -0.5 to 0.5
- w_out: bfloat16 [128, 128], replicated, may hold values from -0.5 to 0.5
- w_back: bfloat16 [128, 768], replicated, may hold values from -0.5 to 0.5
Outputs:
- token_out: bfloat16 [16384, 768], P(('batch', 'seq')), parts along dimension 0
- atom_out: bfloat16 [131072, 128], P(('batch', 'seq')), parts along dimension 0
There are 8 independent parts, one for each index of `batch`. A program takes and returns all parts, laid end to end along the dimension named above; an argument that names none is the same for every part. Nothing has to cross between parts.
Inputs may be any that keep to these rules, and one draw needn't show every extreme that they name: `atom_counts`: every token has at least one atom and the counts of one complex sum to 16384. For every k, the atoms k * 4096 to (k + 1) * 4096 - 1 belong to tokens of (k - 1) * 512 to (k + 2) * 512 - 1.
All inputs are finite; a program needn't handle non-finite values.
Results may differ from a plain program's by a relative error of at most 0.0095.
The roundings to bfloat16 on the way count: a program that leaves them out, or rounds other values in their place, can miss the bound.
Values may be sent and summed in bfloat16 or wider, within the bound.
A program may use at most 128 MiB of HBM per device.

v0:
```python
import functools
import math

import jax
import jax.numpy as jnp
from jax import lax
from jax.experimental import pallas as pl
from jax.experimental.pallas import tpu as pltpu
from jax.sharding import PartitionSpec as P

HEADS = 4
QBLOCK = 32
KEYS = 128
HALO = 48
LANES = 128
MESH = pl.DeviceIdType.MESH
F32 = jnp.float32
BF16 = jnp.bfloat16


def dot(a, b, dims=((1,), (0,))):
    return lax.dot_general(a, b, (dims, ((), ())), preferred_element_type=F32)


def greet(n, me):
    barrier = pltpu.get_barrier_semaphore()
    for d in range(1, n):
        pl.semaphore_signal(barrier, inc=1, device_id={"seq": lax.rem(me + d, n)}, device_id_type=MESH)
    return lambda: pl.semaphore_wait(barrier, n - 1)


def spread(n, atom_rows, cond_ref, wtok_ref, feat_ref, counts_ref, table_ref, halo_ref, ends_ref, starts_ref, wins_ref,
           proj, zeros, cnt, padded, ends_all, send_sem, recv_sem, csend, crecv, lsem):
    me = lax.axis_index("seq")
    tok = cond_ref.shape[0]
    crow = tok // LANES
    right, left = lax.rem(me + 1, n), lax.rem(me + n - 1, n)
    right2, left2 = lax.rem(me + 2, n), lax.rem(me + n - 2, n)

    def remote(i, src, dst, dev):
        return pltpu.make_async_remote_copy(
            src_ref=src, dst_ref=dst, send_sem=send_sem.at[i], recv_sem=recv_sem.at[i],
            device_id={"seq": dev}, device_id_type=MESH)

    arrive = greet(n, me)
    half = tok // 2
    proj[pl.ds(0, half), :] = dot(cond_ref[pl.ds(0, half), :], wtok_ref[...]).astype(BF16)
    arrive()
    ccopies = []
    for d in range(1, n):
        c = pltpu.make_async_remote_copy(
            src_ref=counts_ref, dst_ref=cnt.at[d - 1], send_sem=csend.at[d - 1], recv_sem=crecv.at[d - 1],
            device_id={"seq": lax.rem(me + d, n)}, device_id_type=MESH)
        c.start()
        ccopies.append(c)

    def pair(i, at):
        return [
            remote(i, proj.at[pl.ds(at, half)], table_ref.at[pl.ds(LANES + at, half)], right),
            remote(i + 1, proj.at[pl.ds(at, half)], table_ref.at[pl.ds(LANES + 2 * tok + at, half)], left),
        ]

    copies = pair(0, 0)
    for c in copies:
        c.start()
    proj[pl.ds(half, half), :] = dot(cond_ref[pl.ds(half, half), :], wtok_ref[...]).astype(BF16)
    more = pair(2, half) + [
        remote(4, proj.at[pl.ds(tok - LANES, LANES)], table_ref.at[pl.ds(0, LANES)], right2),
        remote(5, proj.at[pl.ds(0, LANES)], table_ref.at[pl.ds(LANES + 3 * tok, LANES)], left2),
        remote(6, feat_ref.at[pl.ds(atom_rows - HALO, HALO)], halo_ref.at[pl.ds(0, HALO)], right),
        remote(7, feat_ref.at[pl.ds(0, HALO)], halo_ref.at[pl.ds(HALO, HALO)], left),
    ]
    for c in more:
        c.start()
    zeros[...] = jnp.zeros_like(zeros)
    own = pltpu.make_async_copy(proj, table_ref.at[pl.ds(LANES + tok, tok)], lsem.at[0])
    own.start()
    tail = pltpu.make_async_copy(zeros, table_ref.at[pl.ds(2 * LANES + 3 * tok, LANES)], lsem.at[1])
    tail.start()

    padded[...] = jnp.zeros_like(padded)
    rows = padded.shape[0]
    for c in ccopies:
        c.wait()
    for j in range(n):
        part = jnp.where(me == j, counts_ref[...], 0)
        for d in range(1, n):
            part = jnp.where(lax.rem(me + n - d, n) == j, cnt[d - 1], part)
        padded[pl.ds(8 + crow * j, crow), :] = part
    counts = padded[...].astype(F32).astype(BF16)
    tri = (lax.broadcasted_iota(jnp.int32, (LANES, LANES), 0)
           <= lax.broadcasted_iota(jnp.int32, (LANES, LANES), 1)).astype(F32).astype(BF16)
    before = (lax.broadcasted_iota(jnp.int32, (rows, rows), 1)
              < lax.broadcasted_iota(jnp.int32, (rows, rows), 0)).astype(F32).astype(BF16)
    inner = dot(counts, tri)
    outer = jnp.sum(dot(before, counts), axis=1, keepdims=True)
    ends_all[...] = (inner + outer).astype(jnp.int32)
    near = pl.ds(8 - 1 - crow + crow * me, ends_ref.shape[0])
    ends = ends_all[near, :] - me * atom_rows
    ends_ref[...] = ends
    starts_ref[...] = ends - padded[near, :]
    first = jnp.where(lax.broadcasted_iota(jnp.int32, wins_ref.shape, 0) == 0,
                      lax.broadcasted_iota(jnp.int32, wins_ref.shape, 1) * LANES, -HALO)
    w = jnp.zeros_like(first)
    for r in range(ends_ref.shape[0] - 1):
        w += jnp.where(ends[r:r + 1, LANES - 1:] <= first, 1, 0)
    wins_ref[...] = jnp.minimum(w, ends_ref.shape[0] - 3)
    for c in copies + more:
        c.wait()
    own.wait()
    tail.wait()


def atoms(n, group, wins, table, halo, feat, ends_v, starts_v, wq, wk, wv, wout, out, own, sides,
          obuf, wqkv, xs, qs, ks, vs, att, mem, pool, osem):
    me = lax.axis_index("seq")
    atom_rows, width = feat.shape
    tok = own.shape[0]
    head = width // HEADS
    nrow = ends_v.shape[0]
    scale = math.log2(math.e) / math.sqrt(head)
    step = group * LANES
    tiles = atom_rows // LANES
    groups = atom_rows // step
    spare = pool.shape[0] - 2 * LANES

    def store(g):
        at = pl.ds(pl.multiple_of(g * step, step), step)
        return pltpu.make_async_copy(obuf.at[at], out.at[at], osem.at[g])

    def each(f):
        def body(g, c):
            f(g)
            return c
        return body

    for i, w in enumerate((wq, wk, wv)):
        wqkv[:, i * width:(i + 1) * width] = w[...]

    def gather(w, first, f):
        r = f.shape[0]
        ids = first + lax.broadcasted_iota(jnp.int32, (r, LANES), 0)
        parts = []
        for s in range(2):
            lo = starts_v[pl.ds(w + s, 1), :]
            hi = ends_v[pl.ds(w + s, 1), :]
            parts.append(jnp.where((ids >= lo) & (ids < hi), F32(1), F32(0)).astype(BF16))
        member = jnp.concatenate(parts, axis=1)
        rows = dot(member, table[pl.ds(pl.multiple_of(w * LANES, LANES), 2 * LANES), :])
        x = (f.astype(F32) + rows).astype(BF16)
        return member, x

    def keyval(at, qkv, r):
        ks[pl.ds(at, r), :] = qkv[:, width:2 * width].astype(BF16)
        vs[pl.ds(at, r), :] = qkv[:, 2 * width:].astype(BF16)

    for first, at in ((-HALO, 0), (atom_rows, atom_rows + HALO)):
        f = halo[pl.ds(0 if first < 0 else HALO, HALO), :]
        w = wins[1, 0] if first < 0 else wins[0, tiles]
        _, x = gather(w, jnp.int32(first), f)
        keyval(at, dot(x, wqkv[...]), HALO)
    pool[...] = jnp.zeros_like(pool)

    lane = lax.broadcasted_iota(jnp.int32, (1, width), 1)
    hmask = [((lane >= h * head) & (lane < (h + 1) * head)) for h in range(HEADS)]
    hmul = [jnp.where(m, F32(1), F32(0)).astype(BF16) for m in hmask]
    ones = jnp.ones((KEYS, width), BF16)
    total = atom_rows * n
    klane = lax.broadcasted_iota(jnp.int32, (1, KEYS), 1)
    per = LANES // QBLOCK

    def pick(o):
        r = o[(HEADS - 1) * QBLOCK:]
        for h in range(HEADS - 2, -1, -1):
            r = jnp.where(hmask[h], o[h * QBLOCK:(h + 1) * QBLOCK], r)
        return r

    def gathers(g):
        made = []
        for u in range(group):
            a = pl.multiple_of(g * step + u * LANES, LANES)
            made.append((a, *gather(wins[0, g * group + u], a, feat[pl.ds(a, LANES), :])))
        return made

    def project(g, made):
        qkvs = [dot(x, wqkv[...]) for _, _, x in made]
        for (a, member, x), qkv in zip(made, qkvs):
            mem[pl.ds(a, LANES), :] = member
            xs[pl.ds(a, LANES), :] = x
            qs[pl.ds(a, LANES), :] = qkv[:, :width].astype(BF16)
            keyval(pl.multiple_of(a + HALO, 16), qkv, LANES)

    def scored(g, js):
        scores = []
        for j in js:
            at = pl.multiple_of(g * step + j * QBLOCK, QBLOCK)
            q = qs[pl.ds(at, QBLOCK), :]
            qb = jnp.concatenate([q * m for m in hmul], axis=0)
            s = dot(qb, ks[pl.ds(at, KEYS), :], ((1,), (1,)))
            pos = me * atom_rows + at - HALO + klane
            scores.append(jnp.where((pos >= 0) & (pos < total), s, F32(-1e30)))
        return scores

    def soft(scores):
        probs = []
        for s in scores:
            m = jnp.max(s, axis=1, keepdims=True)
            probs.append(jnp.exp2((s - m) * F32(scale)).astype(BF16))
        return probs

    def attend(g, js, probs):
        raw = []
        for j, p in zip(js, probs):
            at = pl.multiple_of(g * step + j * QBLOCK, QBLOCK)
            raw.append(dot(p, jnp.concatenate([vs[pl.ds(at, KEYS), :], ones], axis=1)))
        return [(pick(o[:, :width]) / pick(o[:, width:])).astype(BF16) for o in raw]

    def residual(g):
        at = pl.ds(pl.multiple_of(g * step, step), step)
        y = (xs[at, :].astype(F32) + dot(att[at, :], wout[...])).astype(BF16)
        obuf[at, :] = y
        return y

    def pooled(g, y, real):
        parts = [dot(mem[pl.ds(pl.multiple_of(g * step + u * LANES, LANES), LANES), :],
                     y[u * LANES:(u + 1) * LANES], ((0,), (0,))) for u in range(group)]
        for u, part in enumerate(parts):
            first = jnp.where(real, wins[0, g * group + u] * LANES, spare)
            pool[pl.ds(pl.multiple_of(first, LANES), 2 * LANES), :] += part

    early, late = range(group * per // 2), range(group * per // 2, group * per)
    ahead = 2

    def advance(g, more):
        past = jnp.maximum(g - 1, 0)
        s0 = scored(g, early)
        y = residual(past)
        made = gathers(g + ahead) if more else None
        p0 = soft(s0)
        s1 = scored(g, late)
        pooled(past, y, g > 0)
        o0 = attend(g, early, p0)
        p1 = soft(s1)
        o1 = attend(g, late, p1)
        if more:
            project(g + ahead, made)
        att[pl.ds(pl.multiple_of(g * step, step), step), :] = jnp.concatenate(o0 + o1, axis=0)

        @pl.when(g > 0)
        def _():
            store(past).start()

    lax.fori_loop(0, ahead, each(lambda g: project(g, gathers(g))), 0)
    lax.fori_loop(0, groups - ahead, each(lambda g: advance(g, True)), 0)
    lax.fori_loop(groups - ahead, groups, each(lambda g: advance(g, False)), 0)
    y = residual(groups - 1)
    store(groups - 1).start()
    pooled(groups - 1, y, True)
    own[...] = pool[pl.ds(LANES + tok, tok), :]
    sides[0] = pool[pl.ds(LANES, tok), :].astype(BF16)
    sides[1] = pool[pl.ds(LANES + 2 * tok, tok), :].astype(BF16)
    lax.fori_loop(0, groups, each(lambda g: store(g).wait()), 0)


def merge(n, own_ref, sides_ref, counts_ref, pooled_ref, got, send_sem, recv_sem):
    me = lax.axis_index("seq")
    right, left = lax.rem(me + 1, n), lax.rem(me + n - 1, n)
    greet(n, me)()
    copies = [
        pltpu.make_async_remote_copy(
            src_ref=sides_ref.at[i], dst_ref=got.at[i], send_sem=send_sem.at[i], recv_sem=recv_sem.at[i],
            device_id={"seq": dev}, device_id_type=MESH)
        for i, dev in ((0, left), (1, right))
    ]
    for c in copies:
        c.start()
    cols = [jnp.transpose(jnp.broadcast_to(counts_ref[pl.ds(r, 1), :].astype(F32), (LANES, LANES)))
            for r in range(counts_ref.shape[0])]
    for c in copies:
        c.wait()
    for r, col in enumerate(cols):
        at = pl.ds(r * LANES, LANES)
        sums = own_ref[at, :] + got[0, at, :].astype(F32) + got[1, at, :].astype(F32)
        pooled_ref[at, :] = (sums / col).astype(BF16)


VM = pl.BlockSpec(memory_space=pltpu.VMEM)
ANY = pl.BlockSpec(memory_space=pl.ANY)
HBM = pl.BlockSpec(memory_space=pltpu.HBM)
SM = pl.BlockSpec(memory_space=pltpu.SMEM)


def shards(n, token_cond, atom_feat, atom_counts, w_token, w_query, w_key, w_value, w_out, w_back):
    tok, _ = token_cond.shape
    atom_rows, width = atom_feat.shape
    crow = tok // LANES
    counts = atom_counts.reshape(crow, LANES)
    nrow = 3 * crow + 4
    trows = 3 * tok + 3 * LANES
    S = jax.ShapeDtypeStruct
    DMA = pltpu.SemaphoreType.DMA
    prows = -(-(8 + crow * n + nrow) // 8) * 8
    table, halo, ends, starts, wins = pl.pallas_call(
        functools.partial(spread, n, atom_rows),
        name="spread",
        out_shape=(S((trows, width), BF16), S((2 * HALO, width), BF16),
                   S((nrow, LANES), jnp.int32), S((nrow, LANES), jnp.int32),
                   S((8, LANES), jnp.int32)),
        in_specs=[VM, VM, HBM, VM],
        out_specs=(ANY, ANY, VM, VM, VM),
        scratch_shapes=[
            pltpu.VMEM((tok, width), BF16), pltpu.VMEM((LANES, width), BF16),
            pltpu.VMEM((n - 1, crow, LANES), jnp.int32), pltpu.VMEM((prows, LANES), jnp.int32),
            pltpu.VMEM((prows, LANES), jnp.int32),
            DMA((8,)), DMA((8,)), DMA((n - 1,)), DMA((n - 1,)), DMA((2,)),
        ],
        compiler_params=pltpu.CompilerParams(collective_id=0, has_side_effects=True, vmem_limit_bytes=8 << 20),
    )(token_cond, w_token, atom_feat, counts)
    group = 2
    groups = atom_rows // (group * LANES)
    atom_out, own, sides = pl.pallas_call(
        functools.partial(atoms, n, group),
        name="atoms",
        out_shape=(S((atom_rows, width), BF16), S((tok, width), F32), S((2, tok, width), BF16)),
        in_specs=[SM, VM, VM, VM, VM, VM, VM, VM, VM, VM],
        out_specs=(ANY, VM, VM),
        scratch_shapes=[
            pltpu.VMEM((atom_rows, width), BF16), pltpu.VMEM((width, 3 * width), BF16),
            pltpu.VMEM((atom_rows, width), BF16), pltpu.VMEM((atom_rows, width), BF16),
            pltpu.VMEM((atom_rows + 2 * HALO, width), BF16), pltpu.VMEM((atom_rows + 2 * HALO, width), BF16),
            pltpu.VMEM((atom_rows, width), BF16), pltpu.VMEM((atom_rows, 2 * LANES), BF16),
            pltpu.VMEM((trows + 2 * LANES, width), F32),
            DMA((groups,)),
        ],
        compiler_params=pltpu.CompilerParams(vmem_limit_bytes=24 << 20),
    )(wins, table, halo, atom_feat, ends, starts, w_query, w_key, w_value, w_out)
    pooled = pl.pallas_call(
        functools.partial(merge, n),
        name="merge",
        out_shape=S((tok, width), BF16),
        in_specs=[VM, VM, VM],
        out_specs=VM,
        scratch_shapes=[pltpu.VMEM((2, tok, width), BF16), DMA((2,)), DMA((2,))],
        compiler_params=pltpu.CompilerParams(collective_id=1, has_side_effects=True, vmem_limit_bytes=8 << 20),
    )(own, sides, counts)
    token_out = (
        token_cond.astype(F32) + jnp.dot(pooled, w_back, preferred_element_type=F32)
    ).astype(BF16)
    return (token_out, atom_out)


def solution(mesh):
    both = P(("batch", "seq"), None)
    in_specs = (both, both, P(("batch", "seq")), P(), P(), P(), P(), P(), P())
    return jax.shard_map(
        functools.partial(shards, mesh.shape["seq"]), mesh=mesh, in_specs=in_specs, out_specs=(both, both),
        check_vma=False)
```

profile of v0, /device:TPU:0, one launch (start us, length us, event | category | flops | bytes accessed | tf_op | source)
XLA Modules:
  0.0 38.4 jit_solution(2583165815584819466)
XLA Ops:
  0.6 0.0 copy-start
  0.6 0.0 copy-start.1
  0.7 1.3 %copy-done.1 = bf16[4096,128]{1,0:T(8,128)(2,1)S(1)} copy-done((bf16[4096,128]{1,0:T(8,128)(2,1)S(1)}, bf16[4096,128]{1,0:T(8,128)(2,1)}, u32[]{:S(2)}) %copy-start.1) | copy-done | bytes 1048600
  1.9 0.0 copy-start.3
  1.9 1.1 %copy-done.3 = bf16[512,768]{1,0:T(8,128)(2,1)S(1)} copy-done((bf16[512,768]{1,0:T(8,128)(2,1)S(1)}, bf16[512,768]{1,0:T(8,128)(2,1)}, u32[]{:S(2)}) %copy-start.3) | copy-done | bytes 786456
  3.0 0.0 copy-start.5
  3.0 0.9 %copy-done.5 = bf16[768,128]{1,0:T(8,128)(2,1)S(1)} copy-done((bf16[768,128]{1,0:T(8,128)(2,1)S(1)}, bf16[768,128]{1,0:T(8,128)(2,1)}, u32[]{:S(2)}) %copy-start.5) | copy-done | bytes 196632
  4.0 0.0 copy-start.10
  4.0 0.7 %copy-done.10 = s32[512]{0:T(512)S(1)} copy-done((s32[512]{0:T(512)S(1)}, s32[512]{0:T(512)}, u32[]{:S(2)}) %copy-start.10) | copy-done | bytes 2072
  4.7 0.0 copy-start.2
  4.7 0.0 copy-start.6
  4.7 0.0 copy-start.7
  4.7 0.0 copy-start.8
  4.7 0.0 copy-start.9
  4.7 11.4 %spread.1 = (bf16[1920,128]{1,0:T(8,128)(2,1)S(1)}, bf16[96,128]{1,0:T(8,128)(2,1)S(1)}, s32[16,128]{1,0:T(8,128)S(1)}, s32[16,128]{1,0:T(8,128)S(1)}, s32[8,128]{1,0:T(8,128)S(1)}) custom-call(bf16[512,768]{1,0:T(8,128)(2,1)S(1)} %copy-done.3, bf16[768,128]{1,0:T(8,128)(2,1)S(1)} %copy-done.5, bf16[4096,128]{1,0:T(8,128)(2,1)S(1)} %copy-done.1, ...), custom_call_target="tpu_custom_call" | custom-call | tf_op jit(solution)/shard_map/spread/pallas_call | solution.py:303
  16.1 0.0 copy-start.11
  16.1 0.0 copy-done.2
  16.1 0.0 copy-done.6
  16.1 0.0 copy-done.7
  16.1 0.0 copy-done.8
  16.1 0.0 copy-done.9
  16.1 0.0 copy-start.4
  16.1 12.7 %atoms.1 = (bf16[4096,128]{1,0:T(8,128)(2,1)}, f32[512,128]{1,0:T(8,128)S(1)}, bf16[2,512,128]{2,1,0:T(8,128)(2,1)S(1)}) custom-call(s32[8,128]{1,0:T(8,128)S(1)} %get-tuple-element.10.wins, bf16[1920,128]{1,0:T(8,128)(2,1)S(1)} %get-tuple-element.11.table, bf16[96,128]{1,0:T(8,128)(2,1)S(1)} %get-tuple-element.12.halo, bf16[4096,128]{1,0:T(8,128)(2,1)S(1)} %copy-done.2, ...), custom_call_target="tpu_custom_call" | custom-call | tf_op jit(solution)/shard_map/atoms/pallas_call | solution.py:321
  28.8 0.0 copy-done.11
  28.9 8.2 %merge.1 = bf16[512,128]{1,0:T(8,128)(2,1)S(1)} custom-call(f32[512,128]{1,0:T(8,128)S(1)} %get-tuple-element.15.own_ref, bf16[2,512,128]{2,1,0:T(8,128)(2,1)S(1)} %get-tuple-element.16.sides_ref, s32[4,128]{1,0:T(4,128)S(1)} %bitcast.4), custom_call_target="tpu_custom_call" | custom-call | tf_op jit(solution)/shard_map/merge/pallas_call | solution.py:337
  37.1 0.0 copy-done
  37.1 0.0 copy-done.4
  37.1 1.2 %add_convert_fusion = bf16[512,768]{1,0:T(8,128)(2,1)} fusion(bf16[512,768]{1,0:T(8,128)(2,1)S(1)} %copy-done.4, bf16[512,128]{1,0:T(8,128)(2,1)S(1)} %merge.1, bf16[128,768]{1,0:T(8,128)(2,1)S(1)} %copy-done), kind=kOutput, calls=%fused_computation | convolution fusion | flops 101842944 | bytes 1900544 | tf_op jit(solution)/shard_map/dot_general | solution.py:347
Async XLA Ops:
  0.6 36.5 %copy-start = (bf16[128,768]{1,0:T(8,128)(2,1)S(1)}, bf16[128,768]{1,0:T(8,128)(2,1)}, u32[]{:S(2)}) copy-start(bf16[128,768]{1,0:T(8,128)(2,1)} %param.17) | copy-start | bytes 589828
  0.6 1.3 %copy-start.1 = (bf16[4096,128]{1,0:T(8,128)(2,1)S(1)}, bf16[4096,128]{1,0:T(8,128)(2,1)}, u32[]{:S(2)}) copy-start(bf16[4096,128]{1,0:T(8,128)(2,1)} %feat.1) | copy-start | bytes 3145732
  1.9 1.1 %copy-start.3 = (bf16[512,768]{1,0:T(8,128)(2,1)S(1)}, bf16[512,768]{1,0:T(8,128)(2,1)}, u32[]{:S(2)}) copy-start(bf16[512,768]{1,0:T(8,128)(2,1)} %cond_ref.1) | copy-start | bytes 2359300
  3.0 0.9 %copy-start.5 = (bf16[768,128]{1,0:T(8,128)(2,1)S(1)}, bf16[768,128]{1,0:T(8,128)(2,1)}, u32[]{:S(2)}) copy-start(bf16[768,128]{1,0:T(8,128)(2,1)} %wtok_ref.1) | copy-start | bytes 589828
  4.0 0.7 %copy-start.10 = (s32[512]{0:T(512)S(1)}, s32[512]{0:T(512)}, u32[]{:S(2)}) copy-start(s32[512]{0:T(512)} %param.11) | copy-start | bytes 6148
  4.7 11.4 %copy-start.2 = (bf16[4096,128]{1,0:T(8,128)(2,1)S(1)}, bf16[4096,128]{1,0:T(8,128)(2,1)}, u32[]{:S(2)}) copy-start(bf16[4096,128]{1,0:T(8,128)(2,1)} %feat.1) | copy-start | bytes 3145732
  4.7 11.4 %copy-start.6 = (bf16[128,128]{1,0:T(8,128)(2,1)S(1)}, bf16[128,128]{1,0:T(8,128)(2,1)}, u32[]{:S(2)}) copy-start(bf16[128,128]{1,0:T(8,128)(2,1)} %wq.1) | copy-start | bytes 98308
  4.7 11.4 %copy-start.7 = (bf16[128,128]{1,0:T(8,128)(2,1)S(1)}, bf16[128,128]{1,0:T(8,128)(2,1)}, u32[]{:S(2)}) copy-start(bf16[128,128]{1,0:T(8,128)(2,1)} %wk.1) | copy-start | bytes 98308
  4.7 11.5 %copy-start.8 = (bf16[128,128]{1,0:T(8,128)(2,1)S(1)}, bf16[128,128]{1,0:T(8,128)(2,1)}, u32[]{:S(2)}) copy-start(bf16[128,128]{1,0:T(8,128)(2,1)} %wv.1) | copy-start | bytes 98308
  4.7 11.5 %copy-start.9 = (bf16[128,128]{1,0:T(8,128)(2,1)S(1)}, bf16[128,128]{1,0:T(8,128)(2,1)}, u32[]{:S(2)}) copy-start(bf16[128,128]{1,0:T(8,128)(2,1)} %wout.1) | copy-start | bytes 98308
  16.1 12.8 %copy-start.11 = (s32[512]{0:T(512)S(1)}, s32[512]{0:T(512)}, u32[]{:S(2)}) copy-start(s32[512]{0:T(512)} %param.11) | copy-start | bytes 6148
  16.1 21.0 %copy-start.4 = (bf16[512,768]{1,0:T(8,128)(2,1)S(1)}, bf16[512,768]{1,0:T(8,128)(2,1)}, u32[]{:S(2)}) copy-start(bf16[512,768]{1,0:T(8,128)(2,1)} %cond_ref.1) | copy-start | bytes 2359300
where the time goes:
time: 38.6 us; the launch traced here: 38.4 us
  Pallas kernels  32.3 us (84%)
  local copies, waits for them, and re-layouts  4.04 us (10%)
  matrix products  1.23 us (3%)
  between operations  0.77 us (2%)
    pallas_call x1, Pallas kernels, shards(): pl.pallas_call(functools.partial(atoms, n, group), name='atoms', out_shap...  12.7 us
    pallas_call x1, Pallas kernels, shards(): pl.pallas_call(functools.partial(spread, n, atom_rows), name='spread', ou...  11.4 us
    pallas_call x1, Pallas kernels, shards(): pl.pallas_call(functools.partial(merge, n), name='merge', out_shape=S((to...  8.25 us
    unnamed x24, local copies, waits for them, and re-layouts  4.04 us
    dot_general x1, matrix products, shards(): jnp.dot(pooled, w_back, preferred_element_type=F32)  1.23 us

commit v1 on v0

v1 whole, which is shorter than its diff:
```python
import functools
import math

import jax
import jax.numpy as jnp
from jax import lax
from jax.experimental import pallas as pl
from jax.experimental.pallas import tpu as pltpu
from jax.sharding import PartitionSpec as P

HEADS = 4
QBLOCK = 32
KEYS = 128
HALO = 48
LANES = 128
MESH = pl.DeviceIdType.MESH
F32 = jnp.float32
BF16 = jnp.bfloat16


def dot(a, b, dims=((1,), (0,))):
    return lax.dot_general(a, b, (dims, ((), ())), preferred_element_type=F32)


def greet(n, me):
    barrier = pltpu.get_barrier_semaphore()
    for d in range(1, n):
        pl.semaphore_signal(barrier, inc=1, device_id={"seq": lax.rem(me + d, n)}, device_id_type=MESH)
    return lambda: pl.semaphore_wait(barrier, n - 1)


def whole(n, group, cond_h, wtok_h, feat_h, counts_h, wq_h, wk_h, wv_h, wout_h, obuf, pooled_ref,
          cond, wtok, feat, wqkv, wout, table, halo, cnt, padded, ends_all, ends_v, starts_v, wins_v, wins, cols,
          xs, qs, ks, vs, att, mem, hmem, run, sbuf, got, lsem, csend, crecv, send_sem, recv_sem, ssend, srecv):
    me = lax.axis_index("seq")
    tok = cond.shape[0]
    atom_rows, width = feat.shape
    crow = tok // LANES
    head = width // HEADS
    nrow = ends_v.shape[0]
    scale = math.log2(math.e) / math.sqrt(head)
    step = group * LANES
    tiles = atom_rows // LANES
    groups = atom_rows // step
    right, left = lax.rem(me + 1, n), lax.rem(me + n - 1, n)
    right2, left2 = lax.rem(me + 2, n), lax.rem(me + n - 2, n)

    arrive = greet(n, me)
    loads = [pltpu.make_async_copy(counts_h, cnt.at[me], lsem.at[0]),
             pltpu.make_async_copy(wtok_h, wtok, lsem.at[1])]
    loads += [pltpu.make_async_copy(cond_h.at[pl.ds(r * LANES, LANES)], cond.at[pl.ds(r * LANES, LANES)],
                                    lsem.at[8 + r]) for r in range(crow)]
    loads.append(pltpu.make_async_copy(feat_h, feat, lsem.at[2]))
    loads += [pltpu.make_async_copy(w, wqkv.at[:, pl.ds(i * width, width)], lsem.at[3 + i])
              for i, w in enumerate((wq_h, wk_h, wv_h))]
    loads.append(pltpu.make_async_copy(wout_h, wout, lsem.at[6]))
    for c in loads:
        c.start()

    base = LANES + tok
    table[pl.ds(0, LANES - HALO), :] = jnp.zeros((LANES - HALO, width), BF16)
    table[pl.ds(LANES + 3 * tok + HALO, 2 * LANES - HALO), :] = jnp.zeros((2 * LANES - HALO, width), BF16)
    run[pl.ds(0, 2 * LANES), :] = jnp.zeros((2 * LANES, width), F32)
    padded[...] = jnp.zeros_like(padded)
    loads[1].wait()
    for r in range(crow):
        loads[2 + r].wait()
        table[pl.ds(base + r * LANES, LANES), :] = dot(cond[pl.ds(r * LANES, LANES), :], wtok[...]).astype(BF16)
    loads[0].wait()
    loads[2 + crow].wait()
    arrive()

    ccopies = [pltpu.make_async_remote_copy(
        src_ref=cnt.at[me], dst_ref=cnt.at[me], send_sem=csend.at[d - 1], recv_sem=crecv.at[d - 1],
        device_id={"seq": lax.rem(me + d, n)}, device_id_type=MESH) for d in range(1, n)]

    def remote(i, src, dst, dev):
        return pltpu.make_async_remote_copy(
            src_ref=src, dst_ref=dst, send_sem=send_sem.at[i], recv_sem=recv_sem.at[i],
            device_id={"seq": dev}, device_id_type=MESH)

    copies = [
        remote(0, feat.at[pl.ds(atom_rows - HALO, HALO)], halo.at[pl.ds(0, HALO)], right),
        remote(1, feat.at[pl.ds(0, HALO)], halo.at[pl.ds(HALO, HALO)], left),
        remote(2, table.at[pl.ds(base + tok - HALO, HALO)], table.at[pl.ds(LANES - HALO, HALO)], right2),
        remote(3, table.at[pl.ds(base, HALO)], table.at[pl.ds(LANES + 3 * tok, HALO)], left2),
        remote(4, table.at[pl.ds(base, tok)], table.at[pl.ds(LANES, tok)], right),
        remote(5, table.at[pl.ds(base, tok)], table.at[pl.ds(LANES + 2 * tok, tok)], left),
    ]
    for c in ccopies + copies:
        c.start()

    def column(r):
        return jnp.transpose(jnp.broadcast_to(cnt[me, pl.ds(r, 1), :].astype(F32), (LANES, LANES)))

    for r in range(crow):
        cols[pl.ds(r * LANES, LANES), :] = column(r)
    for c in ccopies:
        c.wait()
    rows = padded.shape[0]
    for j in range(n):
        padded[pl.ds(8 + crow * j, crow), :] = cnt[j]
    counts = padded[...].astype(F32).astype(BF16)
    tri = (lax.broadcasted_iota(jnp.int32, (LANES, LANES), 0)
           <= lax.broadcasted_iota(jnp.int32, (LANES, LANES), 1)).astype(F32).astype(BF16)
    before = (lax.broadcasted_iota(jnp.int32, (rows, rows), 1)
              < lax.broadcasted_iota(jnp.int32, (rows, rows), 0)).astype(F32).astype(BF16)
    inner = dot(counts, tri)
    outer = jnp.sum(dot(before, counts), axis=1, keepdims=True)
    ends_all[...] = (inner + outer).astype(jnp.int32)
    near = pl.ds(8 - 1 - crow + crow * me, nrow)
    ends = ends_all[near, :] - me * atom_rows
    ends_v[...] = ends
    starts_v[...] = ends - padded[near, :]
    sizes = jnp.sum(padded[...], axis=1, keepdims=True)
    start = 8 - 1 - crow + crow * me
    past = lax.broadcasted_iota(jnp.int32, (rows, 1), 0) < start
    mark = jnp.sum(jnp.where(past, sizes, 0), axis=0, keepdims=True) - me * atom_rows
    near_sizes = jnp.sum(padded[near, :], axis=1, keepdims=True)
    first = jnp.where(lax.broadcasted_iota(jnp.int32, (8, LANES), 0) == 0,
                      lax.broadcasted_iota(jnp.int32, (8, LANES), 1) * LANES, -HALO)
    w = jnp.zeros_like(first)
    for r in range(nrow - 1):
        mark = mark + near_sizes[r:r + 1, :]
        w += jnp.where(mark <= first, 1, 0)
    w = jnp.minimum(w, nrow - 3)
    wins_v[pl.ds(0, 8), :] = w
    held = lax.broadcasted_iota(jnp.int32, (1, LANES), 1) < tiles
    w0 = jnp.where(held, w[0:1, :], nrow)
    block = lax.broadcasted_iota(jnp.int32, (nrow, LANES), 0)
    seen = jnp.sum(jnp.where(w0 <= block, 1, 0), axis=1, keepdims=True)
    last = w[0:1, tiles - 1:tiles]
    wins_v[pl.ds(8, nrow), :] = jnp.where(
        block <= last, seen * 2, jnp.where(block == last + 1, 2 * tiles + 1, 0))
    down = pltpu.make_async_copy(wins_v, wins, lsem.at[7])
    down.start()
    down.wait()

    def each(f):
        def body(g, c):
            f(g)
            return c
        return body

    def members(w, first, r):
        ids = first + lax.broadcasted_iota(jnp.int32, (r, LANES), 0)
        parts = []
        for s in range(2):
            lo = starts_v[pl.ds(w + s, 1), :]
            hi = ends_v[pl.ds(w + s, 1), :]
            parts.append(jnp.where((ids >= lo) & (ids < hi), F32(1), F32(0)).astype(BF16))
        return jnp.concatenate(parts, axis=1)

    def gather(w, member, f):
        picked = dot(member, table[pl.ds(w * LANES, 2 * LANES), :])
        return (f.astype(F32) + picked).astype(BF16)

    def build(i):
        a = pl.multiple_of(i * LANES, LANES)
        mem[pl.ds(a, LANES), :] = members(wins[0, i], a, LANES)

    lax.fori_loop(0, tiles, each(build), 0)
    outside = ((-HALO, 0, wins[1, 0]), (atom_rows, atom_rows + HALO, wins[0, tiles]))
    for i, (start, _, w) in enumerate(outside):
        hmem[pl.ds(i * HALO, HALO), :] = members(w, jnp.int32(start), HALO)
    for c in loads[3 + crow:]:
        c.wait()
    for c in copies:
        c.wait()

    def keyval(at, qkv, r):
        ks[pl.ds(at, r), :] = qkv[:, width:2 * width].astype(BF16)
        vs[pl.ds(at, r), :] = qkv[:, 2 * width:].astype(BF16)

    for i, (_, at, w) in enumerate(outside):
        x = gather(w, hmem[pl.ds(i * HALO, HALO), :], halo[pl.ds(i * HALO, HALO), :])
        keyval(at, dot(x, wqkv[...]), HALO)

    lane = lax.broadcasted_iota(jnp.int32, (1, width), 1)
    hmask = [((lane >= h * head) & (lane < (h + 1) * head)) for h in range(HEADS)]
    hmul = [jnp.where(m, F32(1), F32(0)).astype(BF16) for m in hmask]
    ones = jnp.ones((KEYS, width), BF16)
    total = atom_rows * n
    klane = lax.broadcasted_iota(jnp.int32, (1, KEYS), 1)
    per = LANES // QBLOCK

    def pick(o):
        r = o[(HEADS - 1) * QBLOCK:]
        for h in range(HEADS - 2, -1, -1):
            r = jnp.where(hmask[h], o[h * QBLOCK:(h + 1) * QBLOCK], r)
        return r

    def gathers(g):
        made = []
        for u in range(group):
            a = pl.multiple_of(g * step + u * LANES, LANES)
            made.append((a, gather(wins[0, g * group + u], mem[pl.ds(a, LANES), :], feat[pl.ds(a, LANES), :])))
        return made

    def project(made):
        qkvs = [dot(x, wqkv[...]) for _, x in made]
        for (a, x), qkv in zip(made, qkvs):
            xs[pl.ds(a, LANES), :] = x
            qs[pl.ds(a, LANES), :] = qkv[:, :width].astype(BF16)
            keyval(pl.multiple_of(a + HALO, 16), qkv, LANES)

    def scored(g, js):
        scores = []
        for j in js:
            at = pl.multiple_of(g * step + j * QBLOCK, QBLOCK)
            q = qs[pl.ds(at, QBLOCK), :]
            qb = jnp.concatenate([q * m for m in hmul], axis=0)
            s = dot(qb, ks[pl.ds(at, KEYS), :], ((1,), (1,)))
            pos = me * atom_rows + at - HALO + klane
            scores.append(jnp.where((pos >= 0) & (pos < total), s, F32(-1e30)))
        return scores

    def soft(scores):
        probs = []
        for s in scores:
            m = jnp.max(s, axis=1, keepdims=True)
            probs.append(jnp.exp2((s - m) * F32(scale)).astype(BF16))
        return probs

    def attend(g, js, probs):
        raw = []
        for j, p in zip(js, probs):
            at = pl.multiple_of(g * step + j * QBLOCK, QBLOCK)
            raw.append(dot(p, jnp.concatenate([vs[pl.ds(at, KEYS), :], ones], axis=1)))
        return [(pick(o[:, :width]) / pick(o[:, width:])).astype(BF16) for o in raw]

    def residual(g):
        at = pl.ds(pl.multiple_of(g * step, step), step)
        y = (xs[at, :].astype(F32) + dot(att[at, :], wout[...])).astype(BF16)
        obuf[at, :] = y
        return y

    def pooled(g, y):
        parts = [dot(mem[pl.ds(pl.multiple_of(g * step + u * LANES, LANES), LANES), :],
                     y[u * LANES:(u + 1) * LANES], ((0,), (0,))) for u in range(group)]
        at = pl.multiple_of(2 * step * g, 2 * step)
        acc = run[pl.ds(at, 2 * LANES), :]
        for u, part in enumerate(parts):
            i = g * group + u
            same = wins[0, i] == wins[0, jnp.maximum(i - 1, 0)]
            low = jnp.where(same, acc[:LANES], acc[LANES:])
            high = jnp.where(same, acc[LANES:], F32(0))
            acc = part + jnp.concatenate([low, high], axis=0)
            run[pl.ds(pl.multiple_of(at + (u + 1) * 2 * LANES, 2 * LANES), 2 * LANES), :] = acc

    early, late = range(group * per // 2), range(group * per // 2, group * per)
    ahead = 2

    def advance(g, more):
        past = jnp.maximum(g - 1, 0)
        s0 = scored(g, early)
        y = residual(past)
        made = gathers(g + ahead) if more else None
        p0 = soft(s0)
        s1 = scored(g, late)
        pooled(past, y)
        o0 = attend(g, early, p0)
        p1 = soft(s1)
        o1 = attend(g, late, p1)
        if more:
            project(made)
        att[pl.ds(pl.multiple_of(g * step, step), step), :] = jnp.concatenate(o0 + o1, axis=0)

    lax.fori_loop(0, ahead, each(lambda g: project(gathers(g))), 0)
    lax.fori_loop(0, groups - ahead, each(lambda g: advance(g, True)), 0)
    lax.fori_loop(groups - ahead, groups, each(lambda g: advance(g, False)), 0)
    y = residual(groups - 1)
    pooled(groups - 1, y)

    def sums(b):
        return run[pl.ds(wins[8 + b, 0] * LANES, LANES), :]

    sides = []
    for r in range(crow):
        for i, (b, dev) in enumerate(((1 + r, left), (1 + 2 * crow + r, right))):
            at = pl.ds(r * LANES, LANES)
            sbuf[i, at, :] = sums(b).astype(BF16)
            c = pltpu.make_async_remote_copy(
                src_ref=sbuf.at[i, at], dst_ref=got.at[i, at], send_sem=ssend.at[i, r], recv_sem=srecv.at[i, r],
                device_id={"seq": dev}, device_id_type=MESH)
            c.start()
            sides.append(c)
    for r in range(crow):
        for c in sides[2 * r:2 * r + 2]:
            c.wait()
        at = pl.ds(r * LANES, LANES)
        s = sums(1 + crow + r) + got[0, at, :].astype(F32) + got[1, at, :].astype(F32)
        pooled_ref[at, :] = (s / cols[at, :]).astype(BF16)


def finish(atoms_ref, pooled_ref, cond_ref, wback_ref, token_ref, out_ref, tbuf, sem):
    tok = cond_ref.shape[0]
    out = pltpu.make_async_copy(atoms_ref, out_ref, sem.at[0])
    out.start()
    copies = []
    for r in range(tok // LANES):
        at = pl.ds(r * LANES, LANES)
        tbuf[at, :] = (cond_ref[at, :].astype(F32) + dot(pooled_ref[at, :], wback_ref[...])).astype(BF16)
        c = pltpu.make_async_copy(tbuf.at[at], token_ref.at[at], sem.at[1 + r])
        c.start()
        copies.append(c)
    for c in copies:
        c.wait()
    out.wait()


VM = pl.BlockSpec(memory_space=pltpu.VMEM)
ANY = pl.BlockSpec(memory_space=pl.ANY)
HBM = pl.BlockSpec(memory_space=pltpu.HBM)


def shards(n, token_cond, atom_feat, atom_counts, w_token, w_query, w_key, w_value, w_out, w_back):
    tok, ct = token_cond.shape
    atom_rows, width = atom_feat.shape
    crow = tok // LANES
    counts = atom_counts.reshape(crow, LANES)
    nrow = 3 * crow + 4
    trows = 3 * tok + 3 * LANES
    tiles = atom_rows // LANES
    S = jax.ShapeDtypeStruct
    V = pltpu.VMEM
    DMA = pltpu.SemaphoreType.DMA
    prows = -(-(8 + crow * n + nrow) // 8) * 8
    group = 2
    I32 = jnp.int32
    hold = lambda x: pltpu.with_memory_space_constraint(x, pltpu.HBM)
    atoms, pooled = pl.pallas_call(
        functools.partial(whole, n, group),
        name="whole",
        out_shape=(S((atom_rows, width), BF16), S((tok, width), BF16)),
        in_specs=[HBM] * 8,
        out_specs=(VM, VM),
        scratch_shapes=[
            V((tok, ct), BF16), V((ct, width), BF16), V((atom_rows, width), BF16), V((width, 3 * width), BF16),
            V((width, width), BF16), V((trows, width), BF16), V((2 * HALO, width), BF16),
            V((n, crow, LANES), I32), V((prows, LANES), I32), V((prows, LANES), I32),
            V((nrow, LANES), I32), V((nrow, LANES), I32), V((8 + nrow, LANES), I32),
            pltpu.SMEM((8 + nrow, LANES), I32), V((tok, LANES), F32),
            V((atom_rows, width), BF16), V((atom_rows, width), BF16),
            V((atom_rows + 2 * HALO, width), BF16), V((atom_rows + 2 * HALO, width), BF16),
            V((atom_rows, width), BF16), V((atom_rows, 2 * LANES), BF16), V((2 * HALO, 2 * LANES), BF16),
            V(((tiles + 1) * 2 * LANES, width), F32),
            V((2, tok, width), BF16), V((2, tok, width), BF16),
            DMA((8 + crow,)), DMA((n - 1,)), DMA((n - 1,)), DMA((6,)), DMA((6,)), DMA((2, crow)), DMA((2, crow)),
        ],
        compiler_params=pltpu.CompilerParams(collective_id=0, has_side_effects=True, vmem_limit_bytes=24 << 20),
    )(*[hold(x) for x in (token_cond, w_token, atom_feat, counts, w_query, w_key, w_value, w_out)])
    token_out, atom_out = pl.pallas_call(
        finish,
        name="finish",
        out_shape=(S((tok, ct), BF16), S((atom_rows, width), BF16)),
        in_specs=[VM, VM, VM, VM],
        out_specs=(ANY, ANY),
        scratch_shapes=[V((tok, ct), BF16), DMA((1 + crow,))],
        compiler_params=pltpu.CompilerParams(vmem_limit_bytes=8 << 20),
    )(atoms, pooled, token_cond, w_back)
    return (token_out, atom_out)


def solution(mesh):
    both = P(("batch", "seq"), None)
    in_specs = (both, both, P(("batch", "seq")), P(), P(), P(), P(), P(), P())
    return jax.shard_map(
        functools.partial(shards, mesh.shape["seq"]), mesh=mesh, in_specs=in_specs, out_specs=(both, both),
        check_vma=False)
```

time: 38.6 us -> 32.9 us (0.85)
  local copies, waits for them, and re-layouts: 4.04 us -> 0.01 us
  matrix products: 1.23 us -> 0 us
    unnamed x24 -> x4, local copies, waits for them, and re-layouts: 4.04 us -> 0.01 us
    dot_general x1 -> x0, matrix products: 1.23 us -> none  [shards(): jnp.dot(pooled, w_back, preferred_element_type=F32)]
    pallas_call x3 -> x2, Pallas kernels: 32.3 us -> 32.1 us  [the longest x1 30.8 us: shards(): pl.pallas_call(functools.partial(whole, n, group), name='whole', out_shap...]
where the time goes in v1:
time: 32.9 us; the launch traced here: 32.8 us
  Pallas kernels  32.1 us (98%)
  between operations  0.67 us (2%)
    pallas_call x1, Pallas kernels, shards(): pl.pallas_call(functools.partial(whole, n, group), name='whole', out_shap...  30.8 us
    pallas_call x1, Pallas kernels, shards(): pl.pallas_call(finish, name='finish', out_shape=(S((tok, ct), BF16), S((a...  1.27 us

profile of v1, /device:TPU:0, one launch (start us, length us, event | category | flops | bytes accessed | tf_op | source)
XLA Modules:
  0.0 32.8 jit_solution(7893612531777332244)
XLA Ops:
  0.6 0.0 copy-start
  0.6 0.0 copy-start.1
  0.7 30.8 %whole.1 = (bf16[4096,128]{1,0:T(8,128)(2,1)S(1)}, bf16[512,128]{1,0:T(8,128)(2,1)S(1)}) custom-call(bf16[512,768]{1,0:T(8,128)(2,1)} %cond_ref.1, bf16[768,128]{1,0:T(8,128)(2,1)} %wtok_h.1, bf16[4096,128]{1,0:T(8,128)(2,1)} %feat_h.1, s32[4,128]{1,0:T(4,128)} %bitcast.1, bf16[128,128]{1,0:T(8,128)(2,1)} %wq_h.1, bf16[128,128]{1,0:T(8,128)(2,1)} %wk_h.1, ...), custom_call_target="tpu_custom_call" | custom-call | tf_op jit(solution)/shard_map/whole/pallas_call | solution.py:332
  31.5 0.0 copy-done
  31.5 0.0 copy-done.1
  31.5 1.3 %finish.1 = (bf16[512,768]{1,0:T(8,128)(2,1)}, bf16[4096,128]{1,0:T(8,128)(2,1)}) custom-call(bf16[4096,128]{1,0:T(8,128)(2,1)S(1)} %get-tuple-element.4.atoms_ref, bf16[512,128]{1,0:T(8,128)(2,1)S(1)} %get-tuple-element.5.pooled_ref, bf16[512,768]{1,0:T(8,128)(2,1)S(1)} %copy-done, bf16[128,768]{1,0:T(8,128)(2,1)S(1)} %copy-done.1), custom_call_target="tpu_custom_call" | custom-call | tf_op jit(solution)/shard_map/finish/pallas_call | solution.py:353
Async XLA Ops:
  0.6 30.8 %copy-start = (bf16[512,768]{1,0:T(8,128)(2,1)S(1)}, bf16[512,768]{1,0:T(8,128)(2,1)}, u32[]{:S(2)}) copy-start(bf16[512,768]{1,0:T(8,128)(2,1)} %cond_ref.1) | copy-start | bytes 2359300
  0.6 30.8 %copy-start.1 = (bf16[128,768]{1,0:T(8,128)(2,1)S(1)}, bf16[128,768]{1,0:T(8,128)(2,1)}, u32[]{:S(2)}) copy-start(bf16[128,768]{1,0:T(8,128)(2,1)} %wback_ref.1) | copy-start | bytes 589828

commit v2 on v1

--- a/solution.py
+++ b/solution.py
@@ -13,6 +13,7 @@
 KEYS = 128
 HALO = 48
 LANES = 128
+MOST = 24
 MESH = pl.DeviceIdType.MESH
 F32 = jnp.float32
 BF16 = jnp.bfloat16
@@ -45,6 +46,14 @@
     right, left = lax.rem(me + 1, n), lax.rem(me + n - 1, n)
     right2, left2 = lax.rem(me + 2, n), lax.rem(me + n - 2, n)
 
+    odd = lax.rem(me, 2)
+    has_left, has_right = me > 0, me < n - 1
+
+    def blank(at):
+        table[pl.ds(at, tok), :] = jnp.zeros((tok, width), BF16)
+
+    pl.when(me == 0)(lambda: blank(LANES))
+    pl.when(me == n - 1)(lambda: blank(LANES + 2 * tok))
     arrive = greet(n, me)
     loads = [pltpu.make_async_copy(counts_h, cnt.at[me], lsem.at[0]),
              pltpu.make_async_copy(wtok_h, wtok, lsem.at[1])]
@@ -84,11 +93,14 @@
         remote(1, feat.at[pl.ds(0, HALO)], halo.at[pl.ds(HALO, HALO)], left),
         remote(2, table.at[pl.ds(base + tok - HALO, HALO)], table.at[pl.ds(LANES - HALO, HALO)], right2),
         remote(3, table.at[pl.ds(base, HALO)], table.at[pl.ds(LANES + 3 * tok, HALO)], left2),
-        remote(4, table.at[pl.ds(base, tok)], table.at[pl.ds(LANES, tok)], right),
-        remote(5, table.at[pl.ds(base, tok)], table.at[pl.ds(LANES + 2 * tok, tok)], left),
     ]
     for c in ccopies + copies:
         c.start()
+    to_right = remote(4, table.at[pl.ds(base, tok)], table.at[pl.ds(LANES, tok)], right)
+    to_left = remote(5, table.at[pl.ds(base, tok)], table.at[pl.ds(LANES + 2 * tok, tok)], left)
+    pl.when((odd == 1) & has_right)(to_right.start)
+    pl.when(has_left)(to_left.start)
+    pl.when((odd == 0) & has_right)(to_right.start)
 
     def column(r):
         return jnp.transpose(jnp.broadcast_to(cnt[me, pl.ds(r, 1), :].astype(F32), (LANES, LANES)))
@@ -167,6 +179,8 @@
         c.wait()
     for c in copies:
         c.wait()
+    pl.when(has_left)(to_right.wait_recv)
+    pl.when(has_right)(to_left.wait_recv)
 
     def keyval(at, qkv, r):
         ks[pl.ds(at, r), :] = qkv[:, width:2 * width].astype(BF16)
@@ -248,8 +262,23 @@
             acc = part + jnp.concatenate([low, high], axis=0)
             run[pl.ds(pl.multiple_of(at + (u + 1) * 2 * LANES, 2 * LANES), 2 * LANES), :] = acc
 
+    def sums(b):
+        return run[pl.ds(wins[8 + b, 0] * LANES, LANES), :]
+
+    def side(i, dev, r):
+        at = pl.ds(r * LANES, LANES)
+        return pltpu.make_async_remote_copy(
+            src_ref=sbuf.at[i, at], dst_ref=got.at[i, at], send_sem=ssend.at[i, r], recv_sem=srecv.at[i, r],
+            device_id={"seq": dev}, device_id_type=MESH)
+
+    def share(i, dev, r):
+        sbuf[i, pl.ds(r * LANES, LANES), :] = sums(1 + 2 * crow * i + r).astype(BF16)
+        side(i, dev, r).start()
+
     early, late = range(group * per // 2), range(group * per // 2, group * per)
-    ahead = 2
+    ahead = 1
+    ready = min((groups - 1) * step // (MOST * LANES), crow) if ahead == 1 else 0
+
 
     def advance(g, more):
         past = jnp.maximum(g - 1, 0)
@@ -257,13 +286,16 @@
         y = residual(past)
         made = gathers(g + ahead) if more else None
         p0 = soft(s0)
+        if more:
+            project(made)
         s1 = scored(g, late)
         pooled(past, y)
+        if not more:
+            for r in range(ready):
+                pl.when(has_left)(functools.partial(share, 0, left, r))
         o0 = attend(g, early, p0)
         p1 = soft(s1)
         o1 = attend(g, late, p1)
-        if more:
-            project(made)
         att[pl.ds(pl.multiple_of(g * step, step), step), :] = jnp.concatenate(o0 + o1, axis=0)
 
     lax.fori_loop(0, ahead, each(lambda g: project(gathers(g))), 0)
@@ -272,25 +304,24 @@
     y = residual(groups - 1)
     pooled(groups - 1, y)
 
-    def sums(b):
-        return run[pl.ds(wins[8 + b, 0] * LANES, LANES), :]
-
-    sides = []
-    for r in range(crow):
-        for i, (b, dev) in enumerate(((1 + r, left), (1 + 2 * crow + r, right))):
-            at = pl.ds(r * LANES, LANES)
-            sbuf[i, at, :] = sums(b).astype(BF16)
-            c = pltpu.make_async_remote_copy(
-                src_ref=sbuf.at[i, at], dst_ref=got.at[i, at], send_sem=ssend.at[i, r], recv_sem=srecv.at[i, r],
-                device_id={"seq": dev}, device_id_type=MESH)
-            c.start()
-            sides.append(c)
-    for r in range(crow):
-        for c in sides[2 * r:2 * r + 2]:
-            c.wait()
+    for r in range(crow):
+        pl.when((odd == 1) & has_right)(functools.partial(share, 1, right, r))
+    for r in range(ready, crow):
+        pl.when(has_left)(functools.partial(share, 0, left, r))
+    for r in range(crow):
+        pl.when((odd == 0) & has_right)(functools.partial(share, 1, right, r))
+    for r in range(crow):
         at = pl.ds(r * LANES, LANES)
-        s = sums(1 + crow + r) + got[0, at, :].astype(F32) + got[1, at, :].astype(F32)
+        pl.when(has_left)(side(1, right, r).wait_recv)
+        pl.when(has_right)(side(0, left, r).wait_recv)
+        s = (sums(1 + crow + r) + jnp.where(has_right, got[0, at, :].astype(F32), 0)
+             + jnp.where(has_left, got[1, at, :].astype(F32), 0))
         pooled_ref[at, :] = (s / cols[at, :]).astype(BF16)
+    pl.when(has_right)(to_right.wait_send)
+    pl.when(has_left)(to_left.wait_send)
+    for r in range(crow):
+        pl.when(has_right)(side(1, right, r).wait_send)
+        pl.when(has_left)(side(0, left, r).wait_send)
 
 
 def finish(atoms_ref, pooled_ref, cond_ref, wback_ref, token_ref, out_ref, tbuf, sem):
@@ -326,7 +357,7 @@
     V = pltpu.VMEM
     DMA = pltpu.SemaphoreType.DMA
     prows = -(-(8 + crow * n + nrow) // 8) * 8
-    group = 2
+    group = 8
     I32 = jnp.int32
     hold = lambda x: pltpu.with_memory_space_constraint(x, pltpu.HBM)
     atoms, pooled = pl.pallas_call(

time: 32.9 us -> 28.1 us (0.85)
  Pallas kernels: 32.1 us -> 27.2 us
    pallas_call x1, Pallas kernels: 30.8 us -> 26 us  [shards(): pl.pallas_call(functools.partial(whole, n, group), name='whole', out_shap...]
where the time goes in v2:
time: 28.1 us; the launch traced here: 27.9 us
  Pallas kernels  27.2 us (97%)
  between operations  0.67 us (2%)
    pallas_call x1, Pallas kernels, shards(): pl.pallas_call(functools.partial(whole, n, group), name='whole', out_shap...  26 us
    pallas_call x1, Pallas kernels, shards(): pl.pallas_call(finish, name='finish', out_shape=(S((tok, ct), BF16), S((a...  1.27 us

profile of v2, /device:TPU:0, one launch (start us, length us, event | category | flops | bytes accessed | tf_op | source)
XLA Modules:
  0.0 27.9 jit_solution(14246573118859858510)
XLA Ops:
  0.6 0.0 copy-start
  0.6 0.0 copy-start.1
  0.7 26.0 %whole.1 = (bf16[4096,128]{1,0:T(8,128)(2,1)S(1)}, bf16[512,128]{1,0:T(8,128)(2,1)S(1)}) custom-call(bf16[512,768]{1,0:T(8,128)(2,1)} %cond_ref.1, bf16[768,128]{1,0:T(8,128)(2,1)} %wtok_h.1, bf16[4096,128]{1,0:T(8,128)(2,1)} %feat_h.1, s32[4,128]{1,0:T(4,128)} %bitcast.1, bf16[128,128]{1,0:T(8,128)(2,1)} %wq_h.1, bf16[128,128]{1,0:T(8,128)(2,1)} %wk_h.1, ...), custom_call_target="tpu_custom_call" | custom-call | tf_op jit(solution)/shard_map/whole/pallas_call | solution.py:363
  26.6 0.0 copy-done
  26.6 0.0 copy-done.1
  26.7 1.3 %finish.1 = (bf16[512,768]{1,0:T(8,128)(2,1)}, bf16[4096,128]{1,0:T(8,128)(2,1)}) custom-call(bf16[4096,128]{1,0:T(8,128)(2,1)S(1)} %get-tuple-element.4.atoms_ref, bf16[512,128]{1,0:T(8,128)(2,1)S(1)} %get-tuple-element.5.pooled_ref, bf16[512,768]{1,0:T(8,128)(2,1)S(1)} %copy-done, bf16[128,768]{1,0:T(8,128)(2,1)S(1)} %copy-done.1), custom_call_target="tpu_custom_call" | custom-call | tf_op jit(solution)/shard_map/finish/pallas_call | solution.py:384
Async XLA Ops:
  0.6 26.0 %copy-start = (bf16[512,768]{1,0:T(8,128)(2,1)S(1)}, bf16[512,768]{1,0:T(8,128)(2,1)}, u32[]{:S(2)}) copy-start(bf16[512,768]{1,0:T(8,128)(2,1)} %cond_ref.1) | copy-start | bytes 2359300
  0.6 26.0 %copy-start.1 = (bf16[128,768]{1,0:T(8,128)(2,1)S(1)}, bf16[128,768]{1,0:T(8,128)(2,1)}, u32[]{:S(2)}) copy-start(bf16[128,768]{1,0:T(8,128)(2,1)} %wback_ref.1) | copy-start | bytes 589828

commit v3 on v2

--- a/solution.py
+++ b/solution.py
@@ -197,6 +197,7 @@
     total = atom_rows * n
     klane = lax.broadcasted_iota(jnp.int32, (1, KEYS), 1)
     per = LANES // QBLOCK
+    unit = group // 4
 
     def pick(o):
         r = o[(HEADS - 1) * QBLOCK:]
@@ -243,19 +244,19 @@
             raw.append(dot(p, jnp.concatenate([vs[pl.ds(at, KEYS), :], ones], axis=1)))
         return [(pick(o[:, :width]) / pick(o[:, width:])).astype(BF16) for o in raw]
 
-    def residual(g):
-        at = pl.ds(pl.multiple_of(g * step, step), step)
+    def residual(tile):
+        at = pl.ds(pl.multiple_of(tile * LANES, LANES), unit * LANES)
         y = (xs[at, :].astype(F32) + dot(att[at, :], wout[...])).astype(BF16)
         obuf[at, :] = y
         return y
 
-    def pooled(g, y):
-        parts = [dot(mem[pl.ds(pl.multiple_of(g * step + u * LANES, LANES), LANES), :],
-                     y[u * LANES:(u + 1) * LANES], ((0,), (0,))) for u in range(group)]
-        at = pl.multiple_of(2 * step * g, 2 * step)
+    def pooled(tile, y):
+        parts = [dot(mem[pl.ds(pl.multiple_of((tile + u) * LANES, LANES), LANES), :],
+                     y[u * LANES:(u + 1) * LANES], ((0,), (0,))) for u in range(unit)]
+        at = pl.multiple_of(2 * LANES * tile, 2 * LANES)
         acc = run[pl.ds(at, 2 * LANES), :]
         for u, part in enumerate(parts):
-            i = g * group + u
+            i = tile + u
             same = wins[0, i] == wins[0, jnp.maximum(i - 1, 0)]
             low = jnp.where(same, acc[:LANES], acc[LANES:])
             high = jnp.where(same, acc[LANES:], F32(0))
@@ -275,34 +276,51 @@
         sbuf[i, pl.ds(r * LANES, LANES), :] = sums(1 + 2 * crow * i + r).astype(BF16)
         side(i, dev, r).start()
 
-    early, late = range(group * per // 2), range(group * per // 2, group * per)
     ahead = 1
-    ready = min((groups - 1) * step // (MOST * LANES), crow) if ahead == 1 else 0
+    ready = min((tiles - group // 2) // MOST, crow)
 
 
     def advance(g, more):
-        past = jnp.maximum(g - 1, 0)
-        s0 = scored(g, early)
+        start = g * group
+        q = [range(k * unit * per, (k + 1) * unit * per) for k in range(4)]
+
+        def keep(k, p):
+            at = pl.ds(pl.multiple_of((start + k * unit) * LANES, LANES), unit * LANES)
+            att[at, :] = jnp.concatenate(attend(g, q[k], p), axis=0)
+
+        past = jnp.maximum(start - unit, 0)
+        s0 = scored(g, q[0])
         y = residual(past)
         made = gathers(g + ahead) if more else None
+        s1 = scored(g, q[1])
         p0 = soft(s0)
         if more:
             project(made)
-        s1 = scored(g, late)
+        keep(0, p0)
+        s2 = scored(g, q[2])
+        p1 = soft(s1)
         pooled(past, y)
+        y = residual(start)
+        keep(1, p1)
+        s3 = scored(g, q[3])
+        p2 = soft(s2)
+        pooled(start, y)
+        y = residual(start + unit)
+        keep(2, p2)
+        p3 = soft(s3)
+        pooled(start + unit, y)
         if not more:
             for r in range(ready):
                 pl.when(has_left)(functools.partial(share, 0, left, r))
-        o0 = attend(g, early, p0)
-        p1 = soft(s1)
-        o1 = attend(g, late, p1)
-        att[pl.ds(pl.multiple_of(g * step, step), step), :] = jnp.concatenate(o0 + o1, axis=0)
+        y = residual(start + 2 * unit)
+        keep(3, p3)
+        pooled(start + 2 * unit, y)
 
     lax.fori_loop(0, ahead, each(lambda g: project(gathers(g))), 0)
     lax.fori_loop(0, groups - ahead, each(lambda g: advance(g, True)), 0)
     lax.fori_loop(groups - ahead, groups, each(lambda g: advance(g, False)), 0)
-    y = residual(groups - 1)
-    pooled(groups - 1, y)
+    y = residual(tiles - unit)
+    pooled(tiles - unit, y)
 
     for r in range(crow):
         pl.when((odd == 1) & has_right)(functools.partial(share, 1, right, r))
@@ -357,7 +375,7 @@
     V = pltpu.VMEM
     DMA = pltpu.SemaphoreType.DMA
     prows = -(-(8 + crow * n + nrow) // 8) * 8
-    group = 8
+    group = 16
     I32 = jnp.int32
     hold = lambda x: pltpu.with_memory_space_constraint(x, pltpu.HBM)
     atoms, pooled = pl.pallas_call(

time: 28.1 us -> 26.3 us (0.936)
  Pallas kernels: 27.2 us -> 25.5 us
    pallas_call x1, Pallas kernels: 26 us -> 24.2 us  [shards(): pl.pallas_call(functools.partial(whole, n, group), name='whole', out_shap...]
where the time goes in v3:
time: 26.3 us; the launch traced here: 26.1 us
  Pallas kernels  25.5 us (97%)
  between operations  0.67 us (3%)
    pallas_call x1, Pallas kernels, shards(): pl.pallas_call(functools.partial(whole, n, group), name='whole', out_shap...  24.2 us
    pallas_call x1, Pallas kernels, shards(): pl.pallas_call(finish, name='finish', out_shape=(S((tok, ct), BF16), S((a...  1.27 us

profile of v3, /device:TPU:0, one launch (start us, length us, event | category | flops | bytes accessed | tf_op | source)
XLA Modules:
  0.0 26.1 jit_solution(13272692182453047308)
XLA Ops:
  0.6 0.0 copy-start
  0.6 0.0 copy-start.1
  0.7 24.2 %whole.1 = (bf16[4096,128]{1,0:T(8,128)(2,1)S(1)}, bf16[512,128]{1,0:T(8,128)(2,1)S(1)}) custom-call(bf16[512,768]{1,0:T(8,128)(2,1)} %cond_ref.1, bf16[768,128]{1,0:T(8,128)(2,1)} %wtok_h.1, bf16[4096,128]{1,0:T(8,128)(2,1)} %feat_h.1, s32[4,128]{1,0:T(4,128)} %bitcast.1, bf16[128,128]{1,0:T(8,128)(2,1)} %wq_h.1, bf16[128,128]{1,0:T(8,128)(2,1)} %wk_h.1, ...), custom_call_target="tpu_custom_call" | custom-call | tf_op jit(solution)/shard_map/whole/pallas_call | solution.py:381
  24.8 0.0 copy-done
  24.9 0.0 copy-done.1
  24.9 1.3 %finish.1 = (bf16[512,768]{1,0:T(8,128)(2,1)}, bf16[4096,128]{1,0:T(8,128)(2,1)}) custom-call(bf16[4096,128]{1,0:T(8,128)(2,1)S(1)} %get-tuple-element.4.atoms_ref, bf16[512,128]{1,0:T(8,128)(2,1)S(1)} %get-tuple-element.5.pooled_ref, bf16[512,768]{1,0:T(8,128)(2,1)S(1)} %copy-done, bf16[128,768]{1,0:T(8,128)(2,1)S(1)} %copy-done.1), custom_call_target="tpu_custom_call" | custom-call | tf_op jit(solution)/shard_map/finish/pallas_call | solution.py:402
Async XLA Ops:
  0.6 24.2 %copy-start = (bf16[512,768]{1,0:T(8,128)(2,1)S(1)}, bf16[512,768]{1,0:T(8,128)(2,1)}, u32[]{:S(2)}) copy-start(bf16[512,768]{1,0:T(8,128)(2,1)} %cond_ref.1) | copy-start | bytes 2359300
  0.6 24.2 %copy-start.1 = (bf16[128,768]{1,0:T(8,128)(2,1)S(1)}, bf16[128,768]{1,0:T(8,128)(2,1)}, u32[]{:S(2)}) copy-start(bf16[128,768]{1,0:T(8,128)(2,1)} %wback_ref.1) | copy-start | bytes 589828
